TPU v7x, 32 devices: a whole 2x2x4 slice. The times are simulated.
32 devices in a mesh: field: 2 (over x), ep: 16 (over z, y, core).
Axes of the slice: x: 2, y: 2, z: 4, core: 2. Of those that a mesh axis runs over, the one named last changes fastest.
Arguments:
- images: float32 [64, 16, 256], P(('field', 'ep')), parts along dimension 0, may hold values from -6 to 6
- reference_image: float32 [32, 256], P('field'), parts along dimension 0, may hold values from -6 to 6
- kernels: float32 [16, 23, 23], replicated, may hold values from -0.25 to 0.25
- kernel_index: int32 [64], P(('field', 'ep')), parts along dimension 0, may hold values from 0 to 15
- tile_mask: int32 [64, 16, 2], P(('field', 'ep')), parts along dimension 0, may hold values 0 or 1
- systematics: float32 [64, 40], P('field'), parts along dimension 0, may hold values from -6 to 6
- onsets: int32 [16], P('field'), parts along dimension 0, may hold values from 0 to 27
Outputs:
- coefficients: float32 [48, 32, 256], P(None, ('field', 'ep')), parts along dimension 1
- epoch_scatter: float32 [64], P('field'), parts along dimension 0
There are 2 independent parts, one for each index of `field`. A program takes and returns all parts, laid end to end along the dimension named above; an argument that names none is the same for every part. Nothing has to cross between parts.
All inputs are finite; a program needn't handle non-finite values. No bound on the sum of `tile_mask` on one device may be relied on, other than what follows from the above.
Results may differ from a plain program's by a relative error of at most 0.00011.
Values sent between devices are 32-bit elements; how exact they have to be, the bound alone decides.
A program may use at most 64 MiB of HBM per device.

v0:
```python
import math
import jax
import jax.numpy as jnp
from jax import lax
from jax.sharding import PartitionSpec as P

cov_ridge = 0.5
fit_ridge = 1.0


def correlate(stack, chosen):
    count, rows, width = stack.shape
    side = chosen.shape[1]
    half = (side - 1) // 2
    padded = jnp.pad(stack, ((0, 0), (half, half), (half, half)))
    filters = jnp.transpose(chosen, (1, 2, 0))[:, :, None, :]
    strip = math.gcd(rows, 16)

    def one_strip(start):
        piece = lax.dynamic_slice_in_dim(padded, start, strip + 2 * half, 1)
        result = lax.conv_general_dilated(
            piece[None],
            filters,
            (1, 1),
            "VALID",
            dimension_numbers=("NCHW", "HWIO", "NCHW"),
            feature_group_count=count,
            precision=lax.Precision.HIGHEST,
        )
        return result[0]

    starts = jnp.arange(rows // strip, dtype=jnp.int32) * strip
    strips = lax.map(one_strip, starts)
    return jnp.transpose(strips, (1, 0, 2, 3)).reshape(count, rows, width)


def subtract(stack, reference_image, chosen, masks):
    result = reference_image[None] - correlate(stack, chosen)
    shape = result.shape
    tiles = result.reshape(shape[0], shape[1], shape[2] // 128, 128) * masks[..., None].astype(
        jnp.float32
    )
    return tiles.reshape(shape)


def build_design(systematics, onsets):
    count = systematics.shape[0]
    templates = onsets.shape[0]
    epoch_axis = jnp.arange(count, dtype=jnp.float32)[:, None]
    delays = epoch_axis - onsets[None, :].astype(jnp.float32)
    timescale = (jnp.arange(templates, dtype=jnp.float32) + 1.0) * count / (2.0 * templates)
    transient = jnp.where(
        delays >= 0.0, jnp.exp(-jnp.maximum(delays, 0.0) / timescale[None, :]), 0.0
    )
    return jnp.concatenate([systematics, transient], axis=1)


def fit_matrix(scatter, npixels, design):
    count = design.shape[0]
    columns = design.shape[1]
    covariance = scatter / npixels + cov_ridge * jnp.eye(count, dtype=scatter.dtype)
    lower = jnp.linalg.cholesky(covariance)
    weighted = jax.scipy.linalg.cho_solve((lower, True), design)
    normal = jnp.dot(design.T, weighted, precision=lax.Precision.HIGHEST) + fit_ridge * jnp.eye(
        columns, dtype=scatter.dtype
    )
    lower_fit = jnp.linalg.cholesky(normal)
    return jax.scipy.linalg.cho_solve((lower_fit, True), weighted.T)


def shards(images, reference_image, kernels, kernel_index, tile_mask, systematics, onsets):
    local_count, rows, width = images.shape
    basis = kernels.shape[0]
    side = kernels.shape[1]
    onehot = (kernel_index[:, None] == jnp.arange(basis, dtype=jnp.int32)[None, :]).astype(
        jnp.float32
    )
    chosen = jnp.dot(
        onehot, kernels.reshape(basis, side * side), precision=lax.Precision.HIGHEST
    ).reshape(local_count, side, side)
    difference = subtract(images, reference_image, chosen, tile_mask)
    received = lax.all_to_all(difference, "ep", split_axis=1, concat_axis=0, tiled=True)
    count = received.shape[0]
    block_rows = received.shape[1]
    pixel_data = received.reshape(count, block_rows * width)
    partial_value = jnp.dot(pixel_data, pixel_data.T, precision=lax.Precision.HIGHEST)
    scatter = lax.psum(partial_value, "ep")
    npixels = float(rows * width)
    design = build_design(systematics, onsets)
    fit = fit_matrix(scatter, npixels, design)
    coefficients = jnp.dot(fit, pixel_data, precision=lax.Precision.HIGHEST)
    projector = jnp.eye(count, dtype=jnp.float32) - jnp.dot(
        design, fit, precision=lax.Precision.HIGHEST
    )
    product = jnp.dot(projector, scatter, precision=lax.Precision.HIGHEST)
    epoch_scatter = jnp.sum(product * projector, axis=1) / npixels
    return (coefficients.reshape(design.shape[1], block_rows, width), epoch_scatter)


def solution(mesh):
    in_specs = (
        P(("field", "ep"), None, None),
        P("field", None),
        P(),
        P(("field", "ep")),
        P(("field", "ep"), None, None),
        P("field", None),
        P("field"),
    )
    out_specs = (P(None, ("field", "ep"), None), P("field"))
    return jax.shard_map(shards, mesh=mesh, in_specs=in_specs, out_specs=out_specs, check_vma=False)
```

profile of v0, /device:TPU:0, one launch (start us, length us, event | category | flops | bytes accessed | tf_op | source)
XLA Modules:
  0.0 186.9 jit_solution(5411633704186777744)
XLA Ops:
  0.6 0.8 pad_bitcast_fusion
  1.5 0.0 copy-start
  1.5 0.0 copy-start.5
  1.5 0.0 copy-start.4
  1.5 7.8 %copy.30 = f32[1,2,38,278]{1,0,3,2:T(1,128)} copy(f32[1,2,38,278]{3,2,1,0:T(8,128)S(1)} %pad_bitcast_fusion) | data formatting | bytes 169024 | tf_op jit(solution)/shard_map/while/body/eval_jaxpr/broadcast_in_dim | solution.py:22
  9.3 0.0 copy-done
  9.3 0.1 copy.28
  9.3 0.1 reshape.61
  9.5 0.1 dot_general.25
  9.6 0.0 copy-done.5
  9.6 0.2 convolution_bitcast_fusion.1
  9.8 0.3 copy.31
  10.1 0.0 copy-done.4
  10.1 0.7 copy.32
  10.8 0.0 copy-start.2
  10.8 0.0 copy-start.3
  10.8 82.8 %fusion.21 = f32[1,2,16,256]{1,0,3,2:T(1,128)S(1)} fusion(f32[1,2,38,278]{1,0,3,2:T(1,128)} %copy.30, f32[23,23,1,2]{3,2,1,0:T(1,128)S(1)} %copy.31), kind=kOutput, calls=%fused_computation.46 | convolution fusion | flops 52002816 | bytes 121512 | tf_op jit(solution)/shard_map/while/body/eval_jaxpr/conv_general_dilated | solution.py:21
  93.6 0.0 copy-done.2
  93.6 0.0 copy-done.3
  93.6 0.9 bitcast_multiply_fusion
  94.5 0.0 copy-start.6
  94.5 0.0 copy-start.1
  94.5 1.2 copy.33
  95.8 7.4 %all-to-all-start = ((f32[2,16,256]{2,0,1:T(2,128)}), f32[2,16,256]{2,0,1:T(2,128)S(1)}, u32[]{:S(2)}, u32[]{:S(2)}) async-start(f32[2,16,256]{2,0,1:T(2,128)} %copy.33), calls=%async_computation | async-start | bytes 65536 | tf_op jit(solution)/shard_map/all_to_all | solution.py:82
  103.2 0.0 copy-done.6
  103.2 6.6 %all-to-all-done = f32[2,16,256]{2,0,1:T(2,128)S(1)} async-done(((f32[2,16,256]{2,0,1:T(2,128)}), f32[2,16,256]{2,0,1:T(2,128)S(1)}, u32[]{:S(2)}, u32[]{:S(2)}) %all-to-all-start) | async-done | bytes 32800 | tf_op jit(solution)/shard_map/all_to_all | solution.py:82
  109.8 0.2 fusion.22
  110.0 57.7 %psum.7 = f32[32,32]{1,0:T(8,128)S(1)} all-reduce(f32[32,32]{1,0:T(8,128)S(1)} %fusion.22), channel_id=1, replica_groups=mesh['field'=2,'ep'=16] {'ep'}, use_global_device_ids=true, to_apply=%region_0.1 | all-reduce | flops 1024 | bytes 8192 | tf_op jit(solution)/shard_map/psum | solution.py:87
  167.7 0.1 copy.34
  167.8 2.9 %cholesky.34 = f32[32,32]{1,0:T(8,128)S(1)} custom-call(f32[32,32]{1,0:T(8,128)S(1)} %fusion.14), custom_call_target="Cholesky" | custom-call | tf_op jit(solution)/shard_map/jit(cholesky)/cholesky | solution.py:62
  170.7 0.6 compare_reduce_fusion.1
  171.4 0.7 fusion.9
  172.0 2.4 %custom-call.20 = f32[1,32,32]{1,2,0:T(8,128)S(1)} custom-call(f32[1,32,32]{2,1,0:T(8,128)S(1)} %fusion.9), custom_call_target="InvertDiagBlocksLowerTriangular" | custom-call | tf_op jit(solution)/shard_map/jit(_cho_solve)/triangular_solve | solution.py:63
  174.4 0.0 copy-done.1
  174.4 0.3 fusion.12
  174.7 0.1 fusion.10
  174.8 0.3 fusion.20
  175.2 0.1 copy.35
  175.3 4.4 %cholesky.64 = f32[48,48]{1,0:T(8,128)S(1)} custom-call(f32[48,48]{1,0:T(8,128)S(1)} %fusion.8), custom_call_target="Cholesky" | custom-call | tf_op jit(solution)/shard_map/jit(cholesky)/cholesky | solution.py:67
  179.7 0.6 compare_reduce_fusion
  180.3 0.7 fusion.2
  181.0 3.7 %custom-call.21 = f32[1,48,48]{1,2,0:T(8,128)S(1)} custom-call(f32[1,48,48]{2,1,0:T(8,128)S(1)} %fusion.2), custom_call_target="InvertDiagBlocksLowerTriangular" | custom-call | tf_op jit(solution)/shard_map/jit(_cho_solve)/triangular_solve | solution.py:68
  184.7 0.2 fusion.5
  184.8 0.2 fusion.3
  185.0 0.2 convolution_subtract_fusion
  185.2 0.2 convolution_bitcast_fusion
  185.5 0.2 fusion
  185.7 0.5 broadcast_multiply_fusion
  186.2 0.7 copy.38
  (10 shorter events, 0.2 us)
Async XLA Ops:
  1.5 7.8 %copy-start = (f32[16,23,23]{2,0,1:T(8,128)S(1)}, f32[16,23,23]{2,0,1:T(8,128)}, u32[]{:S(2)}) copy-start(f32[16,23,23]{2,0,1:T(8,128)} %param.9) | copy-start | bytes 101572
  1.5 8.1 %copy-start.5 = (s32[2]{0:T(128)S(1)}, s32[2]{0:T(128)}, u32[]{:S(2)}) copy-start(s32[2]{0:T(128)} %param.10) | copy-start | bytes 28
  1.5 8.6 %copy-start.4 = (s32[2,16,2]{1,2,0:T(2,128)S(1)}, s32[2,16,2]{1,2,0:T(2,128)}, u32[]{:S(2)}) copy-start(s32[2,16,2]{1,2,0:T(2,128)} %param.11) | copy-start | bytes 772
  10.8 82.8 %copy-start.2 = (f32[2,16,2]{0,2,1:T(2,128)S(1)}, f32[2,16,2]{0,2,1:T(2,128)}, u32[]{:S(2)}) copy-start(f32[2,16,2]{0,2,1:T(2,128)} %copy.32) | copy-start | bytes 772
  10.8 82.8 %copy-start.3 = (f32[16,256]{1,0:T(8,128)S(1)}, f32[16,256]{1,0:T(8,128)}, u32[]{:S(2)}) copy-start(f32[16,256]{1,0:T(8,128)} %param.8) | copy-start | bytes 49156
  94.5 8.7 %copy-start.6 = (s32[8]{0:T(128)S(1)}, s32[8]{0:T(128)}, u32[]{:S(2)}) copy-start(s32[8]{0:T(128)} %param.13) | copy-start | bytes 100
  94.5 79.9 %copy-start.1 = (f32[32,40]{1,0:T(8,128)S(1)}, f32[32,40]{1,0:T(8,128)}, u32[]{:S(2)}) copy-start(f32[32,40]{1,0:T(8,128)} %param.12) | copy-start | bytes 15364
  95.8 14.1 %all-to-all-start = ((f32[2,16,256]{2,0,1:T(2,128)}), f32[2,16,256]{2,0,1:T(2,128)S(1)}, u32[]{:S(2)}, u32[]{:S(2)}) async-start(f32[2,16,256]{2,0,1:T(2,128)} %copy.33), calls=%async_computation | async-start | bytes 65536 | tf_op jit(solution)/shard_map/all_to_all | solution.py:82
where the time goes:
time: 187 us
  matrix products  84.9 us (45%)
  blocking collectives  57.7 us (31%)
  other arithmetic  17.5 us (9%)
  local copies, waits for them, and re-layouts  12 us (6%)
  starting transfers between devices  7.41 us (4%)
  waiting for transfers between devices  6.57 us (4%)
    conv_general_dilated x1, matrix products, one_strip(): lax.conv_general_dilated(piece[None], filters, (1, 1), 'VALID', dimension...  82.8 us
    psum x1, blocking collectives, shards(): scatter = lax.psum(partial_value, 'ep')  57.7 us
    broadcast_in_dim x2, local copies, waits for them, and re-layouts, one_strip(): piece[None]  8.6 us
    all_to_all x1, starting transfers between devices, shards(): lax.all_to_all(difference, 'ep', split_axis=1, concat_axis=0, tiled=True)  7.41 us
    all_to_all x1, waiting for transfers between devices, shards(): lax.all_to_all(difference, 'ep', split_axis=1, concat_axis=0, tiled=True)  6.57 us
    another operation x3, other arithmetic, fit_matrix(): lower_fit = jnp.linalg.cholesky(normal)  5.05 us
    another operation x2, other arithmetic, fit_matrix(): return jax.scipy.linalg.cho_solve((lower_fit, True), weighted.T)  4.32 us
  transfers between devices with their start and end apart: 1, of which 1 were waited for; matrix products, arithmetic and copies ran while one was open for 0% of the time, Pallas kernels for 0%

commit v1 on v0

--- a/solution.py
+++ b/solution.py
@@ -84,7 +84,9 @@
     block_rows = received.shape[1]
     pixel_data = received.reshape(count, block_rows * width)
     partial_value = jnp.dot(pixel_data, pixel_data.T, precision=lax.Precision.HIGHEST)
-    scatter = lax.psum(partial_value, "ep")
+    scatter = partial_value
+    for hop in (1, 2, 4, 8):
+        scatter = scatter + lax.ppermute(scatter, "ep", [(dev, dev ^ hop) for dev in range(16)])
     npixels = float(rows * width)
     design = build_design(systematics, onsets)
     fit = fit_matrix(scatter, npixels, design)

time: 187 us -> 142 us (0.76)
  blocking collectives: 57.7 us -> 13.8 us
  starting transfers between devices: 7.41 us -> 1.15 us
  waiting for transfers between devices: 6.57 us -> 12.2 us
    psum x1 -> x0, blocking collectives: 57.7 us -> none  [shards(): scatter = lax.psum(partial_value, 'ep')]
    all_to_all x0 -> x1, blocking collectives: none -> 13.8 us  [shards(): lax.all_to_all(difference, 'ep', split_axis=1, concat_axis=0, tiled=True)]
    ppermute x0 -> x4, waiting for transfers between devices: none -> 12.2 us  [shards(): lax.ppermute(scatter, 'ep', [(dev, dev ^ hop) for dev in range(16)])]
    all_to_all x1 -> x0, starting transfers between devices: 7.41 us -> none  [shards(): lax.all_to_all(difference, 'ep', split_axis=1, concat_axis=0, tiled=True)]
    all_to_all x1 -> x0, waiting for transfers between devices: 6.57 us -> none  [shards(): lax.all_to_all(difference, 'ep', split_axis=1, concat_axis=0, tiled=True)]
  transfers between devices with their start and end apart: 1 -> 4, of which waited for: 1 -> 4; matrix products, arithmetic and copies ran while one was open for 0% -> 0% of each run, Pallas kernels for 0% -> 0%
where the time goes in v1:
time: 142 us
  matrix products  84.9 us (60%)
  other arithmetic  17.5 us (12%)
  blocking collectives  13.8 us (10%)
  waiting for transfers between devices  12.2 us (9%)
  local copies, waits for them, and re-layouts  11.4 us (8%)
    conv_general_dilated x1, matrix products, one_strip(): lax.conv_general_dilated(piece[None], filters, (1, 1), 'VALID', dimension...  82.8 us
    all_to_all x1, blocking collectives, shards(): lax.all_to_all(difference, 'ep', split_axis=1, concat_axis=0, tiled=True)  13.8 us
    ppermute x4, waiting for transfers between devices, shards(): lax.ppermute(scatter, 'ep', [(dev, dev ^ hop) for dev in range(16)])  12.2 us
    broadcast_in_dim x2, local copies, waits for them, and re-layouts, one_strip(): piece[None]  8.6 us
    another operation x3, other arithmetic, fit_matrix(): lower_fit = jnp.linalg.cholesky(normal)  5.05 us
    another operation x2, other arithmetic, fit_matrix(): return jax.scipy.linalg.cho_solve((lower_fit, True), weighted.T)  4.32 us
    another operation x3, other arithmetic, fit_matrix(): lower = jnp.linalg.cholesky(covariance)  3.59 us
    another operation x2, other arithmetic, fit_matrix(): weighted = jax.scipy.linalg.cho_solve((lower, True), design)  3.09 us
  transfers between devices with their start and end apart: 4, of which 4 were waited for; matrix products, arithmetic and copies ran while one was open for 0% of the time, Pallas kernels for 0%

profile of v1, /device:TPU:0, one launch (start us, length us, event | category | flops | bytes accessed | tf_op | source)
XLA Modules:
  0.0 141.8 jit_solution(17648449316400826952)
XLA Ops:
  0.6 0.8 pad_bitcast_fusion
  1.5 0.0 copy-start
  1.5 0.0 copy-start.5
  1.5 0.0 copy-start.4
  1.5 7.8 %copy.30 = f32[1,2,38,278]{1,0,3,2:T(1,128)} copy(f32[1,2,38,278]{3,2,1,0:T(8,128)S(1)} %pad_bitcast_fusion) | data formatting | bytes 169024 | tf_op jit(solution)/shard_map/while/body/eval_jaxpr/broadcast_in_dim | solution.py:22
  9.3 0.0 copy-done
  9.3 0.1 copy.28
  9.3 0.1 reshape.61
  9.5 0.1 dot_general.25
  9.6 0.0 copy-done.5
  9.6 0.2 convolution_bitcast_fusion.1
  9.8 0.3 copy.31
  10.1 0.0 copy-done.4
  10.1 0.7 copy.32
  10.8 0.0 copy-start.2
  10.8 0.0 copy-start.3
  10.8 82.8 %fusion.21 = f32[1,2,16,256]{1,0,3,2:T(1,128)S(1)} fusion(f32[1,2,38,278]{1,0,3,2:T(1,128)} %copy.30, f32[23,23,1,2]{3,2,1,0:T(1,128)S(1)} %copy.31), kind=kOutput, calls=%fused_computation.46 | convolution fusion | flops 52002816 | bytes 121512 | tf_op jit(solution)/shard_map/while/body/eval_jaxpr/conv_general_dilated | solution.py:21
  93.6 0.0 copy-done.2
  93.6 0.0 copy-done.3
  93.6 0.9 bitcast_multiply_fusion
  94.5 0.0 copy-start.6
  94.5 0.0 copy-start.1
  94.5 0.6 copy.33
  95.1 13.8 %all_to_all.15 = f32[2,16,256]{2,0,1:T(2,128)S(1)} all-to-all(f32[2,16,256]{2,0,1:T(2,128)S(1)} %copy.33), channel_id=1, replica_groups=mesh['field'=2,'ep'=16] {'ep'}, dimensions={1} | all-to-all | bytes 65536 | tf_op jit(solution)/shard_map/all_to_all | solution.py:82
  109.0 0.2 fusion.22
  109.2 0.1 collective-permute-start
  109.3 1.2 collective-permute-done
  110.4 0.3 collective-permute-start.1
  110.8 3.4 %collective-permute-done.1 = f32[32,32]{1,0:T(8,128)S(1)} collective-permute-done((f32[32,32]{1,0:T(8,128)S(1)}, f32[32,32]{1,0:T(8,128)S(1)}, u32[]{:S(2)}, u32[]{:S(2)}) %collective-permute-start.1) | collective-permute-done | bytes 4128 | tf_op jit(solution)/shard_map/ppermute | solution.py:89
  114.2 0.3 collective-permute-start.2
  114.5 0.0 copy-done.6
  114.5 3.4 %collective-permute-done.2 = f32[32,32]{1,0:T(8,128)S(1)} collective-permute-done((f32[32,32]{1,0:T(8,128)S(1)}, f32[32,32]{1,0:T(8,128)S(1)}, u32[]{:S(2)}, u32[]{:S(2)}) %collective-permute-start.2) | collective-permute-done | bytes 4128 | tf_op jit(solution)/shard_map/ppermute | solution.py:89
  117.9 0.4 collective-permute-start.3
  118.3 4.2 %collective-permute-done.3 = f32[32,32]{1,0:T(8,128)S(1)} collective-permute-done((f32[32,32]{1,0:T(8,128)S(1)}, f32[32,32]{1,0:T(8,128)S(1)}, u32[]{:S(2)}, u32[]{:S(2)}) %collective-permute-start.3) | collective-permute-done | bytes 4128 | tf_op jit(solution)/shard_map/ppermute | solution.py:89
  122.6 0.1 copy.34
  122.7 2.9 %cholesky.34 = f32[32,32]{1,0:T(8,128)S(1)} custom-call(f32[32,32]{1,0:T(8,128)S(1)} %fusion.14), custom_call_target="Cholesky" | custom-call | tf_op jit(solution)/shard_map/jit(cholesky)/cholesky | solution.py:62
  125.6 0.6 compare_reduce_fusion.1
  126.3 0.7 fusion.9
  126.9 2.4 %custom-call.20 = f32[1,32,32]{1,2,0:T(8,128)S(1)} custom-call(f32[1,32,32]{2,1,0:T(8,128)S(1)} %fusion.9), custom_call_target="InvertDiagBlocksLowerTriangular" | custom-call | tf_op jit(solution)/shard_map/jit(_cho_solve)/triangular_solve | solution.py:63
  129.4 0.0 copy-done.1
  129.4 0.3 fusion.12
  129.6 0.1 fusion.10
  129.8 0.3 fusion.20
  130.1 0.1 copy.35
  130.2 4.4 %cholesky.64 = f32[48,48]{1,0:T(8,128)S(1)} custom-call(f32[48,48]{1,0:T(8,128)S(1)} %fusion.8), custom_call_target="Cholesky" | custom-call | tf_op jit(solution)/shard_map/jit(cholesky)/cholesky | solution.py:67
  134.6 0.6 compare_reduce_fusion
  135.2 0.7 fusion.2
  135.9 3.7 %custom-call.21 = f32[1,48,48]{1,2,0:T(8,128)S(1)} custom-call(f32[1,48,48]{2,1,0:T(8,128)S(1)} %fusion.2), custom_call_target="InvertDiagBlocksLowerTriangular" | custom-call | tf_op jit(solution)/shard_map/jit(_cho_solve)/triangular_solve | solution.py:68
  139.6 0.2 fusion.5
  139.7 0.2 fusion.3
  139.9 0.2 convolution_subtract_fusion
  140.1 0.2 convolution_bitcast_fusion
  140.4 0.2 fusion
  140.6 0.5 broadcast_multiply_fusion
  141.1 0.7 copy.38
  (13 shorter events, 0.2 us)
Async XLA Ops:
  1.5 7.8 %copy-start = (f32[16,23,23]{2,0,1:T(8,128)S(1)}, f32[16,23,23]{2,0,1:T(8,128)}, u32[]{:S(2)}) copy-start(f32[16,23,23]{2,0,1:T(8,128)} %param.9) | copy-start | bytes 101572
  1.5 8.1 %copy-start.5 = (s32[2]{0:T(128)S(1)}, s32[2]{0:T(128)}, u32[]{:S(2)}) copy-start(s32[2]{0:T(128)} %param.10) | copy-start | bytes 28
  1.5 8.6 %copy-start.4 = (s32[2,16,2]{1,2,0:T(2,128)S(1)}, s32[2,16,2]{1,2,0:T(2,128)}, u32[]{:S(2)}) copy-start(s32[2,16,2]{1,2,0:T(2,128)} %param.11) | copy-start | bytes 772
  10.8 82.8 %copy-start.2 = (f32[2,16,2]{0,2,1:T(2,128)S(1)}, f32[2,16,2]{0,2,1:T(2,128)}, u32[]{:S(2)}) copy-start(f32[2,16,2]{0,2,1:T(2,128)} %copy.32) | copy-start | bytes 772
  10.8 82.8 %copy-start.3 = (f32[16,256]{1,0:T(8,128)S(1)}, f32[16,256]{1,0:T(8,128)}, u32[]{:S(2)}) copy-start(f32[16,256]{1,0:T(8,128)} %param.8) | copy-start | bytes 49156
  94.5 20.0 %copy-start.6 = (s32[8]{0:T(128)S(1)}, s32[8]{0:T(128)}, u32[]{:S(2)}) copy-start(s32[8]{0:T(128)} %param.13) | copy-start | bytes 100
  94.5 34.8 %copy-start.1 = (f32[32,40]{1,0:T(8,128)S(1)}, f32[32,40]{1,0:T(8,128)}, u32[]{:S(2)}) copy-start(f32[32,40]{1,0:T(8,128)} %param.12) | copy-start | bytes 15364
  109.2 1.2 collective-permute-start
  110.4 3.7 %collective-permute-start.1 = (f32[32,32]{1,0:T(8,128)S(1)}, f32[32,32]{1,0:T(8,128)S(1)}, u32[]{:S(2)}, u32[]{:S(2)}) collective-permute-start(f32[32,32]{1,0:T(8,128)S(1)} %add.65), channel_id=1, source_target_pairs={{0,2},{1,3},{2,0},{3,1},{4,6},{5,7},{6,4},{7,5},{8,10},{9,11},{10,... | collective-permute-start | bytes 12296 | tf_op jit(solution)/shard_map/ppermute | solution.py:89
  114.2 3.7 %collective-permute-start.2 = (f32[32,32]{1,0:T(8,128)S(1)}, f32[32,32]{1,0:T(8,128)S(1)}, u32[]{:S(2)}, u32[]{:S(2)}) collective-permute-start(f32[32,32]{1,0:T(8,128)S(1)} %add.66), channel_id=1, source_target_pairs={{0,4},{1,5},{2,6},{3,7},{4,0},{5,1},{6,2},{7,3},{8,12},{9,13},{10,... | collective-permute-start | bytes 12296 | tf_op jit(solution)/shard_map/ppermute | solution.py:89
  117.9 4.6 %collective-permute-start.3 = (f32[32,32]{1,0:T(8,128)S(1)}, f32[32,32]{1,0:T(8,128)S(1)}, u32[]{:S(2)}, u32[]{:S(2)}) collective-permute-start(f32[32,32]{1,0:T(8,128)S(1)} %add.67), channel_id=1, source_target_pairs={{0,8},{1,9},{2,10},{3,11},{4,12},{5,13},{6,14},{7,15},{8,0},{9,1},... | collective-permute-start | bytes 12296 | tf_op jit(solution)/shard_map/ppermute | solution.py:89
